TPU v7x, 512 devices: a whole 4x8x8 slice. The times are simulated.
512 devices in a mesh: seq: 128 (over y, z, core), head: 4 (over x).
Axes of the slice: x: 4, y: 8, z: 8, core: 2. Of those that a mesh axis runs over, the one named last changes fastest.
Arguments:
- queries: bfloat16 [16384, 1536], P('seq', 'head'), may hold values from -400 to 400
- latent: bfloat16 [16384, 320], P(('seq', 'head')), may hold values from -6 to 6
- w_kv_up: bfloat16 [256, 2048], P(None, 'head'), may hold values from -0.375 to 0.375
Outputs:
- attended: bfloat16 [16384, 1024], P('seq', 'head')
All inputs are finite; a program needn't handle non-finite values.
Results may differ from a plain program's by a relative error of at most 0.004.
Values may be sent and summed in bfloat16 or wider, within the bound.
No kernel may reach another device: no remote copies, remote signals or barrier semaphores. Data moves between devices by JAX's collectives and lax.ppermute only.
A program may use at most 64 MiB of HBM per device.

v0:
```python
import math
import jax
import jax.numpy as jnp
from jax import lax
from jax.sharding import PartitionSpec as P

D_LATENT = 256
ROPE = 64
NOPE = 128
VDIM = 128
MASKED = -1e30


def from_everyone(shard, axis):
    copies = jnp.broadcast_to(shard, (lax.axis_size(axis), *shard.shape))
    return lax.all_to_all(copies, axis, split_axis=0, concat_axis=0, tiled=True)


def joined_along(tiles, dim):
    tiles = jnp.moveaxis(tiles, 0, dim)
    dims = tiles.shape
    return tiles.reshape(*dims[:dim], dims[dim] * dims[dim + 1], *dims[dim + 2 :])


def gathered_copies(shard, axis, dim):
    tiles = from_everyone(shard, axis)
    return joined_along(tiles, dim)


def attend(state, key_block, key_start, setup):
    query_side, query_rope, query_pos, w_kv_up, absorb = setup
    numerator, running_max, totals = state
    key_count = key_block.shape[0]
    highest = lax.Precision.HIGHEST
    key_latent = key_block[:, :D_LATENT]
    key_rope = key_block[:, D_LATENT:]
    scores = jnp.einsum(
        "qhd,kd->hqk", query_side, key_latent.astype(jnp.float32), precision=highest
    )
    scores = scores + jnp.einsum(
        "qhd,kd->hqk", query_rope, key_rope, preferred_element_type=jnp.float32
    )
    scores = scores * (NOPE + ROPE) ** (-0.5)
    key_pos = key_start + lax.iota(jnp.int32, key_count)
    allowed = (key_pos[None, :] <= query_pos[:, None]) & (key_pos[None, :] >= 0)
    scores = jnp.where(allowed[None], scores, MASKED)
    new_max = jnp.maximum(running_max, jnp.max(scores, axis=2))
    factor = jnp.exp(running_max - new_max)
    weights = jnp.where(allowed[None], jnp.exp(scores - new_max[:, :, None]), 0.0)
    totals = totals * factor + jnp.sum(weights, axis=2)
    rounded = weights.astype(jnp.bfloat16)
    update = jnp.einsum("hqk,kd->hqd", rounded, key_latent, preferred_element_type=jnp.float32)
    numerator = numerator * factor[:, :, None] + update
    return (numerator, new_max, totals)


def attend_blocks(state, keys, setup):
    key_total = keys.shape[0]
    block_rows = math.gcd(key_total, 1024)
    block_count = key_total // block_rows

    def one_block(block_index, inner):
        offset = block_index * block_rows
        piece = lax.dynamic_slice_in_dim(keys, offset, block_rows, 0)
        return attend(inner, piece, offset, setup)

    return lax.fori_loop(0, block_count, one_block, state)


def prepare(query_rows, query_pos, w_kv_up):
    row_count = query_rows.shape[0]
    local_heads = w_kv_up.shape[1] // (NOPE + VDIM)
    query_all = query_rows.reshape(row_count, local_heads, NOPE + ROPE)
    w_key = w_kv_up.reshape(D_LATENT, local_heads, NOPE + VDIM)[:, :, :NOPE]
    query_side = jnp.einsum(
        "qhn,dhn->qhd", query_all[:, :, :NOPE], w_key, preferred_element_type=jnp.float32
    )
    width = D_LATENT
    setup = (query_side, query_all[:, :, NOPE:], query_pos, w_kv_up, True)
    start_state = (
        jnp.zeros((local_heads, row_count, width), jnp.float32),
        jnp.full((local_heads, row_count), MASKED, jnp.float32),
        jnp.zeros((local_heads, row_count), jnp.float32),
    )
    return (setup, start_state)


def finish(state, w_kv_up):
    numerator, running_max, totals = state
    local_heads = w_kv_up.shape[1] // (NOPE + VDIM)
    row_count = totals.shape[1]
    w_value = w_kv_up.reshape(D_LATENT, local_heads, NOPE + VDIM)[:, :, NOPE:].astype(jnp.float32)
    numerator = jnp.einsum("hqd,dhv->hqv", numerator, w_value, precision=lax.Precision.HIGHEST)
    result = numerator / totals[:, :, None]
    return (
        jnp.transpose(result, (1, 0, 2)).reshape(row_count, local_heads * VDIM).astype(jnp.bfloat16)
    )


def body(queries, latent, w_kv_up):
    group_rows = queries.shape[0]
    group_index = lax.axis_index("seq")
    query_pos = group_index * group_rows + lax.iota(jnp.int32, group_rows)
    setup, state = prepare(queries, query_pos, w_kv_up)
    gathered = gathered_copies(latent, "head", 0)
    state = attend_blocks(state, lax.all_gather(gathered, "seq", axis=0, tiled=True), setup)
    return finish(state, w_kv_up)


def solution(mesh):
    in_specs = (P("seq", "head"), P(("seq", "head"), None), P(None, "head"))
    out_specs = P("seq", "head")
    return jax.shard_map(body, mesh=mesh, in_specs=in_specs, out_specs=out_specs, check_vma=False)
```

profile of v0, /device:TPU:1, one launch (start us, length us, event | category | flops | bytes accessed | tf_op | source)
XLA Modules:
  0.0 202.9 jit_solution(14311295889934789337)
XLA Ops:
  7.3 9.4 %all_to_all.5 = bf16[4,32,320]{2,1,0:T(8,128)(2,1)} all-to-all(bf16[4,32,320]{2,1,0:T(8,128)(2,1)S(1)} %broadcast_in_dim.69), channel_id=1, replica_groups=mesh['seq'=128,'head'=4] {'head'}, dimensions={0} | all-to-all | bytes 163840 | tf_op jit(solution)/shard_map/all_to_all | solution.py:16
  19.2 93.8 %all-gather.2.cloned.1.call-done = bf16[16384,320]{1,0:T(8,128)(2,1)} async-done(((bf16[128,320]{1,0:T(8,128)(2,1)}), bf16[16384,320]{1,0:T(8,128)(2,1)}) %all-gather.2.cloned.1.call-update) | async-done | bytes 10485776 | tf_op jit(solution)/shard_map/all_gather | solution.py:106
  113.0 82.0 %while.18 = (s32[]{:T(128)}, f32[2,128,256]{2,1,0:T(8,128)S(1)}, f32[2,128]{1,0:T(2,128)S(1)}, f32[2,128]{1,0:T(2,128)S(1)}, bf16[16384,320]{1,0:T(8,128)(2,1)},...) while((s32[]{:T(128)}, f32[2,128,256]{2,1,0:T(8,128)S(1)}, ...), condition=%wide.region_3.4_spmd.clone, body=%wide.region_0.3_spmd.clone.sunk | while | flops 976163200 | bytes 7924967 | solution.py:67
  114.6 1.7 fusion.38
  119.7 1.7 fusion.38
  121.7 1.5 convolution_add_fusion.3
  124.8 1.7 fusion.38
  130.0 1.7 fusion.38
  135.1 1.7 fusion.38
  137.1 1.5 convolution_add_fusion.3
  140.2 1.7 fusion.38
  145.4 1.7 fusion.38
  150.5 1.7 fusion.38
  152.4 1.5 convolution_add_fusion.3
  155.6 1.7 fusion.38
  160.7 1.7 fusion.38
  165.9 1.7 fusion.38
  167.8 1.5 convolution_add_fusion.3
  171.0 1.7 fusion.38
  176.1 1.7 fusion.38
  181.2 1.7 fusion.38
  183.2 1.5 convolution_add_fusion.3
  186.4 1.7 fusion.38
  191.5 1.7 fusion.38
  (168 shorter events, 50.1 us)
Async XLA Ops:
  6.5 106.5 %all-gather.2.cloned.1.call-start = ((), (), s32[]{:S(2)}) async-start(), calls=%async_computation.1 | async-start | bytes 12681216 | tf_op jit(solution)/shard_map/all_gather | solution.py:106
Sparse Core Ops, SparseCore 0:
  16.8 96.1 all-gather.1
where the time goes:
time: 205 us; the launch traced here: 203 us
  waiting for transfers between devices  93.8 us (46%)
  matrix products  71.6 us (35%)
  between operations  13.5 us (7%)
  other arithmetic  9.62 us (5%)
  blocking collectives  9.39 us (5%)
  local copies, waits for them, and re-layouts  3.76 us (2%)
    all_gather x1, waiting for transfers between devices, body(): lax.all_gather(gathered, 'seq', axis=0, tiled=True)  93.8 us
    dot_general x16, matrix products, attend(): jnp.einsum('qhd,kd->hqk', query_side, key_latent.astype(jnp.float32), pre...  27.3 us
    dot_general x16, matrix products, attend(): jnp.einsum('hqk,kd->hqd', rounded, key_latent, preferred_element_type=jnp...  24.2 us
    dot_general x16, matrix products, attend(): jnp.einsum('qhd,kd->hqk', query_rope, key_rope, preferred_element_type=jn...  19.6 us
    all_to_all x1, blocking collectives, from_everyone(): return lax.all_to_all(copies, axis, split_axis=0, concat_axis=0, tiled=True)  9.39 us
    and x16, other arithmetic, attend(): allowed = (key_pos[None, :] <= query_pos[:, None]) & (key_pos[None, :] >= 0)  5.39 us
  transfers between devices with their start and end apart: 1, of which 1 were waited for; matrix products, arithmetic and copies ran while one was open for 1% of the time, Pallas kernels for 0%

commit v1 on v0

--- a/solution.py
+++ b/solution.py
@@ -103,7 +103,13 @@
     query_pos = group_index * group_rows + lax.iota(jnp.int32, group_rows)
     setup, state = prepare(queries, query_pos, w_kv_up)
     gathered = gathered_copies(latent, "head", 0)
-    state = attend_blocks(state, lax.all_gather(gathered, "seq", axis=0, tiled=True), setup)
+    state = attend_blocks(
+        state,
+        jnp.concatenate(
+            lax.all_to_all(jnp.stack([gathered] * lax.axis_size("seq")), "seq", 0, 0), axis=0
+        ),
+        setup,
+    )
     return finish(state, w_kv_up)
 
 

time: 205 us -> 461 us (2.25)
  the two profiles are of different devices: /device:TPU:1 before, /device:TPU:105 now
where the time goes in v1:
time: 461 us; the launch traced here: 458 us
  waiting for transfers between devices  325 us (70%)
  matrix products  71.6 us (16%)
  local copies, waits for them, and re-layouts  23.6 us (5%)
  starting transfers between devices  18.7 us (4%)
  other arithmetic  9.62 us (2%)
  blocking collectives  8.47 us (2%)
    all_to_all x1, waiting for transfers between devices, body(): lax.all_to_all(jnp.stack([gathered] * lax.axis_size('seq')), 'seq', 0, 0)  325 us
    dot_general x16, matrix products, attend(): jnp.einsum('qhd,kd->hqk', query_side, key_latent.astype(jnp.float32), pre...  27.3 us
    dot_general x16, matrix products, attend(): jnp.einsum('hqk,kd->hqd', rounded, key_latent, preferred_element_type=jnp...  24.3 us
    dot_general x16, matrix products, attend(): jnp.einsum('qhd,kd->hqk', query_rope, key_rope, preferred_element_type=jn...  19.5 us
    all_to_all x1, starting transfers between devices, body(): lax.all_to_all(jnp.stack([gathered] * lax.axis_size('seq')), 'seq', 0, 0)  18.7 us
    unnamed x8, local copies, waits for them, and re-layouts  15.4 us
  transfers between devices with their start and end apart: 1, of which 1 were waited for; matrix products, arithmetic and copies ran while one was open for 0% of the time, Pallas kernels for 0%

profile of v1, /device:TPU:105, one launch (start us, length us, event | category | flops | bytes accessed | tf_op | source)
XLA Modules:
  0.0 458.5 jit_solution(10054707968017435752)
XLA Ops:
  0.7 8.5 %all_to_all.10 = bf16[4,32,320]{2,1,0:T(8,128)(2,1)S(1)} all-to-all(bf16[4,32,320]{2,1,0:T(8,128)(2,1)S(1)} %broadcast_in_dim.69), channel_id=1, replica_groups=mesh['seq'=128,'head'=4] {'head'}, dimensions={0} | all-to-all | bytes 163840 | tf_op jit(solution)/shard_map/all_to_all | solution.py:16
  9.3 6.6 %stack.3 = bf16[128,128,320]{1,2,0:T(8,128)(2,1)} broadcast(bf16[128,320]{0,1:T(8,128)(2,1)S(1)} %copy.29), dimensions={1,2} | broadcast | bytes 10567680 | tf_op jit(solution)/shard_map/stack | solution.py:109
  15.9 18.7 %all-to-all-start.1 = ((bf16[128,128,320]{1,2,0:T(8,128)(2,1)}), bf16[128,128,320]{1,2,0:T(8,128)(2,1)}, u32[]{:S(2)}, u32[]{:S(2)}) async-start(bf16[128,128,320]{1,2,0:T(8,128)(2,1)} %stack.3), calls=%async_computation.1 | async-start | bytes 20971520 | tf_op jit(solution)/shard_map/all_to_all | solution.py:109
  35.4 325.0 %all-to-all-done.1 = bf16[128,128,320]{1,2,0:T(8,128)(2,1)} async-done(((bf16[128,128,320]{1,2,0:T(8,128)(2,1)}), bf16[128,128,320]{1,2,0:T(8,128)(2,1)}, u32[]{:S(2)}, u32[]{:S(2)}) %all-to-all-start.1) | async-done | bytes 10485792 | tf_op jit(solution)/shard_map/all_to_all | solution.py:109
  360.4 15.0 %copy.40 = bf16[128,128,320]{2,1,0:T(8,128)(2,1)} copy(bf16[128,128,320]{1,2,0:T(8,128)(2,1)} %all-to-all-done.1) | data formatting | bytes 20971520
  375.4 82.0 %while.18 = (s32[]{:T(128)}, f32[2,128,256]{2,1,0:T(8,128)S(1)}, f32[2,128]{1,0:T(2,128)S(1)}, f32[2,128]{1,0:T(2,128)S(1)}, bf16[16384,320]{1,0:T(8,128)(2,1)},...) while((s32[]{:T(128)}, f32[2,128,256]{2,1,0:T(8,128)S(1)}, ...), condition=%wide.region_3.4_spmd.clone, body=%wide.region_0.3_spmd.clone.sunk | while | flops 976163200 | bytes 7924967 | solution.py:67
  377.0 1.7 fusion.38
  379.0 1.5 convolution_add_fusion.3
  382.1 1.7 fusion.38
  387.3 1.7 fusion.38
  392.4 1.7 fusion.38
  394.4 1.5 convolution_add_fusion.3
  397.5 1.7 fusion.38
  402.6 1.7 fusion.38
  407.8 1.7 fusion.38
  412.9 1.7 fusion.38
  418.0 1.7 fusion.38
  423.2 1.7 fusion.38
  428.3 1.7 fusion.38
  433.4 1.7 fusion.38
  438.5 1.7 fusion.38
  443.7 1.7 fusion.38
  448.8 1.7 fusion.38
  453.9 1.7 fusion.38
  (174 shorter events, 52.9 us)
Async XLA Ops:
  15.9 18.7 %copy-start = (bf16[256,512]{1,0:T(8,128)(2,1)S(1)}, bf16[256,512]{1,0:T(8,128)(2,1)}, u32[]{:S(2)}) copy-start(bf16[256,512]{1,0:T(8,128)(2,1)} %param.7) | copy-start | bytes 786436
  15.9 18.9 %copy-start.1 = (bf16[128,384]{1,0:T(8,128)(2,1)S(1)}, bf16[128,384]{1,0:T(8,128)(2,1)}, u32[]{:S(2)}) copy-start(bf16[128,384]{1,0:T(8,128)(2,1)} %param.5) | copy-start | bytes 294916
  15.9 344.5 %all-to-all-start.1 = ((bf16[128,128,320]{1,2,0:T(8,128)(2,1)}), bf16[128,128,320]{1,2,0:T(8,128)(2,1)}, u32[]{:S(2)}, u32[]{:S(2)}) async-start(bf16[128,128,320]{1,2,0:T(8,128)(2,1)} %stack.3), calls=%async_computation.1 | async-start | bytes 20971520 | tf_op jit(solution)/shard_map/all_to_all | solution.py:109
